TPU v7x, 32 devices: a whole 2x2x4 slice. The times are simulated.
32 devices in a mesh: af: 4 (over y, x), sa: 8 (over z, core).
Axes of the slice: x: 2, y: 2, z: 4, core: 2. Of those that a mesh axis runs over, the one named last changes fastest.
Arguments:
- data_real: bfloat16 [64, 512, 512], P('af', 'sa'), may hold values from -0.5 to 0.5
- data_imaginary: bfloat16 [64, 512, 512], P('af', 'sa'), may hold values from -0.5 to 0.5
- wavelet_real: float32 [64], P('af'), may hold values from -2.5 to 2.5
- wavelet_imaginary: float32 [64], P('af'), may hold values from -2.5 to 2.5
- primaries_real: float32 [64, 512, 512], P('af', 'sa'), may hold values from -3 to 3
- primaries_imaginary: float32 [64, 512, 512], P('af', 'sa'), may hold values from -3 to 3
Outputs:
- updated_real: float32 [64, 512, 512], P('af', 'sa')
- updated_imaginary: float32 [64, 512, 512], P('af', 'sa')
- misfit: float32 [2], replicated
All inputs are finite; a program needn't handle non-finite values.
Results may differ from a plain program's by a relative error of at most 0.0018.
Values may be sent and summed in bfloat16 or wider, within the bound.
A program may use at most 128 MiB of HBM per device.

v0:
```python
import math
import jax
import jax.numpy as jnp
from jax import lax
from jax.sharding import PartitionSpec as P

N = 512
F = 64
ITERS = 2
STEP_LENGTH = 0.02
THRESHOLD = 0.25


def fourier_tables(row_index, col_index):
    phase = row_index[:, None] * col_index[None, :] % F
    angle = phase.astype(jnp.float32) * (2.0 * math.pi / F)
    factor = 1.0 / math.sqrt(F)
    return (jnp.cos(angle) * factor, jnp.sin(angle) * factor)


def highest(left, right):
    return jnp.dot(left, right, precision=lax.Precision.HIGHEST, preferred_element_type=jnp.float32)


def stacked(part_real, part_imaginary):
    return jnp.concatenate(
        [part_real.astype(jnp.bfloat16), part_imaginary.astype(jnp.bfloat16)], axis=1
    )


def shrink(values):
    return values - jnp.clip(values, -THRESHOLD, THRESHOLD)


def on_device(
    data_real, data_imaginary, wavelet_real, wavelet_imaginary, primaries_real, primaries_imaginary
):
    row_count = data_real.shape[1]
    wave_real = wavelet_real[:, None, None]
    wave_imaginary = wavelet_imaginary[:, None, None]
    current_real = primaries_real
    current_imaginary = primaries_imaginary
    own_real = data_real.astype(jnp.float32)
    own_imaginary = data_imaginary.astype(jnp.float32)
    whole_real, whole_imaginary = (
        lax.all_gather(data_real, "sa", axis=1, tiled=True),
        lax.all_gather(data_imaginary, "sa", axis=1, tiled=True),
    )
    local_sums = []
    for iteration in range(ITERS):
        left_rows = stacked(current_real, current_imaginary)
        product_real = jnp.einsum(
            "frk,fkc->frc", left_rows, whole_real, preferred_element_type=jnp.float32
        )
        product_imaginary = jnp.einsum(
            "frk,fkc->frc", left_rows, whole_imaginary, preferred_element_type=jnp.float32
        )
        forward_real = product_real[:, :row_count] - product_imaginary[:, row_count:]
        forward_imaginary = product_imaginary[:, :row_count] + product_real[:, row_count:]
        error_real = (
            own_real
            + forward_real
            - (wave_real * current_real - wave_imaginary * current_imaginary)
        )
        error_imaginary = (
            own_imaginary
            + forward_imaginary
            - (wave_real * current_imaginary + wave_imaginary * current_real)
        )
        local_sum = jnp.sum(error_real * error_real) + jnp.sum(error_imaginary * error_imaginary)
        local_sums.append(local_sum)
        error_rows = stacked(error_real, error_imaginary)
        with_real = jnp.einsum(
            "frk,fjk->frj", error_rows, whole_real, preferred_element_type=jnp.float32
        )
        with_imaginary = jnp.einsum(
            "frk,fjk->frj", error_rows, whole_imaginary, preferred_element_type=jnp.float32
        )
        back_real = with_real[:, :row_count] + with_imaginary[:, row_count:]
        back_imaginary = with_real[:, row_count:] - with_imaginary[:, :row_count]
        gradient_real = wave_real * error_real + wave_imaginary * error_imaginary - back_real
        gradient_imaginary = (
            wave_real * error_imaginary - wave_imaginary * error_real - back_imaginary
        )
        stepped_real = current_real + STEP_LENGTH * gradient_real
        stepped_imaginary = current_imaginary + STEP_LENGTH * gradient_imaginary
        trace_real, trace_imaginary = (
            lax.all_to_all(stepped_real, "af", split_axis=2, concat_axis=0, tiled=True),
            lax.all_to_all(stepped_imaginary, "af", split_axis=2, concat_axis=0, tiled=True),
        )
        block_shape = trace_real.shape
        flat_real = trace_real.reshape(F, -1)
        flat_imaginary = trace_imaginary.reshape(F, -1)
        every_index = jnp.arange(F, dtype=jnp.int32)
        cosine, sine = fourier_tables(every_index, every_index)
        time_real = highest(cosine, flat_real) - highest(sine, flat_imaginary)
        time_imaginary = highest(sine, flat_real) + highest(cosine, flat_imaginary)
        shrunk_real = shrink(time_real)
        shrunk_imaginary = shrink(time_imaginary)
        freq_real = (highest(cosine, shrunk_real) + highest(sine, shrunk_imaginary)).reshape(
            block_shape
        )
        freq_imaginary = (highest(cosine, shrunk_imaginary) - highest(sine, shrunk_real)).reshape(
            block_shape
        )
        current_real, current_imaginary = (
            lax.all_to_all(freq_real, "af", split_axis=0, concat_axis=2, tiled=True),
            lax.all_to_all(freq_imaginary, "af", split_axis=0, concat_axis=2, tiled=True),
        )
    totals = lax.psum(jnp.stack(local_sums), ("af", "sa"))
    misfit = totals / (F * N * N)
    return (current_real, current_imaginary, misfit)


def solution(mesh):
    in_specs = (
        P("af", "sa", None),
        P("af", "sa", None),
        P("af"),
        P("af"),
        P("af", "sa", None),
        P("af", "sa", None),
    )
    out_specs = (P("af", "sa", None), P("af", "sa", None), P())
    return jax.shard_map(
        on_device, mesh=mesh, in_specs=in_specs, out_specs=out_specs, check_vma=False
    )
```

profile of v0, /device:TPU:0, one launch (start us, length us, event | category | flops | bytes accessed | tf_op | source)
XLA Modules:
  0.0 607.2 jit_solution(6934212573473681621)
XLA Ops:
  12.5 81.9 %all-gather.5.cloned.1.call-done = bf16[16,512,512]{2,1,0:T(8,128)(2,1)} async-done(((bf16[16,64,512]{2,1,0:T(8,128)(2,1)}), bf16[16,512,512]{2,1,0:T(8,128)(2,1)}) %all-gather.5.cloned.1.call-update) | async-done | bytes 8388624 | tf_op jit(solution)/shard_map/all_gather | solution.py:47
  94.4 7.3 %fusion.46 = f32[16,128,512]{2,1,0:T(8,128)} fusion(bf16[16,512,512]{2,1,0:T(8,128)(2,1)} %all-gather.5.cloned.1.call-done, bf16[16,64,512]{2,1,0:T(8,128)(2,1)} %convert_element_type.67, bf16[16,64,512]{2,1,0:T(8,128)(2,1)} %convert_element_type.66), kind=kOutput, calls=%fused_computation.88 | convolution fusion | flops 1077936128 | bytes 14680064 | tf_op jit(solution)/shard_map/frk,fkc->frc/dot_general | solution.py:55
  101.6 74.9 %all-gather.3.cloned.1.call-done = bf16[16,512,512]{2,1,0:T(8,128)(2,1)} async-done(((bf16[16,64,512]{2,1,0:T(8,128)(2,1)}), bf16[16,512,512]{2,1,0:T(8,128)(2,1)}) %all-gather.3.cloned.1.call-update) | async-done | bytes 8388624 | tf_op jit(solution)/shard_map/all_gather | solution.py:46
  176.5 5.4 fusion.47
  189.1 6.8 %fusion.44 = f32[16,128,512]{2,1,0:T(8,128)} fusion(bf16[16,512,512]{2,1,0:T(8,128)(2,1)S(1)} %bitcast.119, bf16[16,64,512]{2,1,0:T(8,128)(2,1)} %convert_element_type.70, bf16[16,64,512]{2,1,0:T(8,128)(2,1)} %convert_element_type.69), kind=kOutput, calls=%fused_computation.86 | convolution fusion | flops 1077936128 | bytes 14680064 | tf_op jit(solution)/shard_map/frk,fjk->frj/dot_general | solution.py:76
  195.9 6.5 %fusion.45 = f32[16,128,512]{2,1,0:T(8,128)} fusion(bf16[16,512,512]{2,1,0:T(8,128)(2,1)S(1)} %bitcast.123, bf16[16,64,512]{2,1,0:T(8,128)(2,1)} %convert_element_type.70, bf16[16,64,512]{2,1,0:T(8,128)(2,1)} %convert_element_type.69), kind=kOutput, calls=%fused_computation.87 | convolution fusion | flops 1077936128 | bytes 14680064 | tf_op jit(solution)/shard_map/frk,fjk->frj/dot_general | solution.py:73
  202.5 5.8 fusion.24
  208.3 4.9 copy.19
  213.2 5.5 reshape.44
  222.3 4.9 copy.21
  227.1 5.5 reshape.46
  232.6 15.1 %all-to-all-done = f32[4,1,131072]{2,1,0:T(1,128)S(1)} async-done(((f32[4,1,131072]{2,1,0:T(1,128)}), f32[4,1,131072]{2,1,0:T(1,128)S(1)}, u32[]{:S(2)}, u32[]{:S(2)}) %all-to-all-start) | async-done | bytes 2097184 | tf_op jit(solution)/shard_map/all_to_all | solution.py:88
  249.1 4.9 all-to-all-start.1
  254.5 7.6 %reduce = f32[4,131072]{1,0:T(4,128)S(1)} reduce(f32[4,1,131072]{2,1,0:T(1,128)} %copy-done.27, f32[]{:T(128)} %broadcast.92), dimensions={1}, to_apply=%all_to_all.96.reduce_sub_computation | reduce | bytes 4194308 | tf_op jit(solution)/shard_map/all_to_all | solution.py:88
  278.7 7.6 %reduce.1 = f32[4,131072]{1,0:T(4,128)S(1)} reduce(f32[4,1,131072]{2,1,0:T(1,128)} %all-to-all-done.1, f32[]{:T(128)} %broadcast.92), dimensions={1}, to_apply=%all_to_all.99.reduce_sub_computation | reduce | bytes 4194308 | tf_op jit(solution)/shard_map/all_to_all | solution.py:89
  293.8 4.9 clamp_subtract_fusion.2
  319.4 16.8 %all-to-all-done.3 = f32[64,64,128]{2,1,0:T(8,128)S(1)} async-done(((f32[64,64,128]{2,1,0:T(8,128)}), f32[64,64,128]{2,1,0:T(8,128)S(1)}, u32[]{:S(2)}, u32[]{:S(2)}) %all-to-all-start.3) | async-done | bytes 2097184 | tf_op jit(solution)/shard_map/all_to_all | solution.py:108
  341.8 23.3 %all-to-all-done.2 = f32[64,64,128]{2,1,0:T(8,128)} async-done(((f32[64,64,128]{2,1,0:T(8,128)}), f32[64,64,128]{2,1,0:T(8,128)}, u32[]{:S(2)}, u32[]{:S(2)}) %all-to-all-start.2) | async-done | bytes 2097184 | tf_op jit(solution)/shard_map/all_to_all | solution.py:107
  367.1 4.9 fusion.42
  381.0 6.4 %fusion.40 = f32[16,128,512]{2,1,0:T(8,128)} fusion(bf16[16,512,512]{2,1,0:T(8,128)(2,1)S(1)} %bitcast.121, bf16[16,64,512]{2,1,0:T(8,128)(2,1)} %convert_element_type.74, bf16[16,64,512]{2,1,0:T(8,128)(2,1)} %convert_element_type.73), kind=kOutput, calls=%fused_computation.82 | convolution fusion | flops 1077936128 | bytes 14680064 | tf_op jit(solution)/shard_map/frk,fjk->frj/dot_general | solution.py:76
  387.4 6.5 %fusion.41 = f32[16,128,512]{2,1,0:T(8,128)} fusion(bf16[16,512,512]{2,1,0:T(8,128)(2,1)S(1)} %bitcast.125, bf16[16,64,512]{2,1,0:T(8,128)(2,1)} %convert_element_type.74, bf16[16,64,512]{2,1,0:T(8,128)(2,1)} %convert_element_type.73), kind=kOutput, calls=%fused_computation.83 | convolution fusion | flops 1077936128 | bytes 14680064 | tf_op jit(solution)/shard_map/frk,fjk->frj/dot_general | solution.py:73
  393.9 5.1 bitcast_add_fusion
  399.0 4.9 copy.25
  403.8 5.5 reshape.48
  412.9 4.9 copy.27
  417.8 5.5 reshape.50
  423.3 13.9 %all-to-all-done.4 = f32[4,1,131072]{2,1,0:T(1,128)S(1)} async-done(((f32[4,1,131072]{2,1,0:T(1,128)}), f32[4,1,131072]{2,1,0:T(1,128)S(1)}, u32[]{:S(2)}, u32[]{:S(2)}) %all-to-all-start.4) | async-done | bytes 2097184 | tf_op jit(solution)/shard_map/all_to_all | solution.py:88
  443.3 7.6 %reduce.2 = f32[4,131072]{1,0:T(4,128)S(1)} reduce(f32[4,1,131072]{2,1,0:T(1,128)} %copy-done.28, f32[]{:T(128)} %broadcast.92), dimensions={1}, to_apply=%all_to_all.110.reduce_sub_computation | reduce | bytes 4194308 | tf_op jit(solution)/shard_map/all_to_all | solution.py:88
  467.7 7.6 %reduce.3 = f32[4,131072]{1,0:T(4,128)S(1)} reduce(f32[4,1,131072]{2,1,0:T(1,128)} %all-to-all-done.5, f32[]{:T(128)} %broadcast.92), dimensions={1}, to_apply=%all_to_all.113.reduce_sub_computation | reduce | bytes 4194308 | tf_op jit(solution)/shard_map/all_to_all | solution.py:89
  482.5 4.9 clamp_subtract_fusion
  507.5 18.5 %all-to-all-done.6 = f32[64,64,128]{2,1,0:T(8,128)} async-done(((f32[64,64,128]{2,1,0:T(8,128)}), f32[64,64,128]{2,1,0:T(8,128)}, u32[]{:S(2)}, u32[]{:S(2)}) %all-to-all-start.6) | async-done | bytes 2097184 | tf_op jit(solution)/shard_map/all_to_all | solution.py:107
  532.2 54.3 %psum.7 = f32[2]{0:T(128)S(1)} all-reduce(f32[2]{0:T(128)S(1)} %pad_maximum_fusion.12), channel_id=1, replica_groups=mesh['af'=4,'sa'=8] {'af','sa'}, use_global_device_ids=true, to_apply=%region_4.5 | all-reduce | flops 2 | bytes 16 | tf_op jit(solution)/shard_map/psum | solution.py:110
  (140 shorter events, 149.9 us)
Async XLA Ops:
  7.2 87.2 %all-gather.5.cloned.1.call-start = ((), (), s32[]{:S(2)}) async-start(), calls=%async_computation.9 | async-start | bytes 9437184 | tf_op jit(solution)/shard_map/all_gather | solution.py:47
  7.9 168.6 %all-gather.3.cloned.1.call-start = ((), (), s32[]{:S(2)}) async-start(), calls=%async_computation.8 | async-start | bytes 9437184 | tf_op jit(solution)/shard_map/all_gather | solution.py:46
  101.6 80.3 %copy-start.29 = (f32[16]{0:T(128)S(1)}, f32[16]{0:T(128)}, u32[]{:S(2)}) copy-start(f32[16]{0:T(128)} %param.9) | copy-start | bytes 196
  101.6 80.4 %copy-start.30 = (f32[16]{0:T(128)S(1)}, f32[16]{0:T(128)}, u32[]{:S(2)}) copy-start(f32[16]{0:T(128)} %param.8) | copy-start | bytes 196
  176.5 5.5 copy-start
  176.5 5.9 copy-start.9
  176.5 6.1 %copy-start.21 = (bf16[16,64,512]{2,1,0:T(8,128)(2,1)S(1)}, bf16[16,64,512]{2,1,0:T(8,128)(2,1)}, u32[]{:S(2)}) copy-start(bf16[16,64,512]{2,1,0:T(8,128)(2,1)} %param.7) | copy-start | bytes 3145732
  176.5 6.4 %copy-start.23 = (bf16[16,64,512]{2,1,0:T(8,128)(2,1)S(1)}, bf16[16,64,512]{2,1,0:T(8,128)(2,1)}, u32[]{:S(2)}) copy-start(bf16[16,64,512]{2,1,0:T(8,128)(2,1)} %param.6) | copy-start | bytes 3145732
  176.5 12.5 %slice-start = ((s8[8388608]{0:T(1024)(128)(4,1)}), s8[4194304]{0:T(1024)(128)(4,1)S(1)}, s32[]{:S(2)}) async-start(s8[8388608]{0:T(1024)(128)(4,1)} %bitcast.118), calls=%async_computation.10 | async-start | bytes 8388608
  182.9 6.1 %slice-start.1 = ((s8[8388608]{0:T(1024)(128)(4,1)}), s8[4194304]{0:T(1024)(128)(4,1)S(1)}, s32[]{:S(2)}) async-start(s8[8388608]{0:T(1024)(128)(4,1)} %bitcast.118), calls=%async_computation.11 | async-start | bytes 8388608
  187.9 8.0 %slice-start.4 = ((s8[8388608]{0:T(1024)(128)(4,1)}), s8[4194304]{0:T(1024)(128)(4,1)S(1)}, s32[]{:S(2)}) async-start(s8[8388608]{0:T(1024)(128)(4,1)} %bitcast.122), calls=%async_computation.14 | async-start | bytes 8388608
  189.0 6.8 %slice-start.5 = ((s8[8388608]{0:T(1024)(128)(4,1)}), s8[4194304]{0:T(1024)(128)(4,1)S(1)}, s32[]{:S(2)}) async-start(s8[8388608]{0:T(1024)(128)(4,1)} %bitcast.122), calls=%async_computation.15 | async-start | bytes 8388608
  195.9 6.6 %copy-start.10 = (f32[16,64,512]{2,1,0:T(8,128)S(1)}, f32[16,64,512]{2,1,0:T(8,128)}, u32[]{:S(2)}) copy-start(f32[16,64,512]{2,1,0:T(8,128)} %param.10) | copy-start | bytes 6291460
  195.9 6.6 %copy-start.16 = (f32[16,64,512]{2,1,0:T(8,128)S(1)}, f32[16,64,512]{2,1,0:T(8,128)}, u32[]{:S(2)}) copy-start(f32[16,64,512]{2,1,0:T(8,128)} %copy-done.15) | copy-start | bytes 6291460
  195.9 6.5 %copy-start.18 = (f32[16,64,512]{2,1,0:T(8,128)S(1)}, f32[16,64,512]{2,1,0:T(8,128)}, u32[]{:S(2)}) copy-start(f32[16,64,512]{2,1,0:T(8,128)} %copy-done.17) | copy-start | bytes 6291460
  218.7 29.1 %all-to-all-start = ((f32[4,1,131072]{2,1,0:T(1,128)}), f32[4,1,131072]{2,1,0:T(1,128)S(1)}, u32[]{:S(2)}, u32[]{:S(2)}) async-start(f32[4,1,131072]{2,1,0:T(1,128)} %reshape.44), calls=%async_computation | async-start | bytes 4194304 | tf_op jit(solution)/shard_map/all_to_all | solution.py:88
  249.1 29.6 %all-to-all-start.1 = ((f32[4,1,131072]{2,1,0:T(1,128)}), f32[4,1,131072]{2,1,0:T(1,128)}, u32[]{:S(2)}, u32[]{:S(2)}) async-start(f32[4,1,131072]{2,1,0:T(1,128)} %reshape.46), calls=%async_computation.1 | async-start | bytes 4194304 | tf_op jit(solution)/shard_map/all_to_all | solution.py:89
  302.0 6.0 copy-start.7
  308.0 28.2 %all-to-all-start.3 = ((f32[64,64,128]{2,1,0:T(8,128)}), f32[64,64,128]{2,1,0:T(8,128)S(1)}, u32[]{:S(2)}, u32[]{:S(2)}) async-start(f32[64,64,128]{2,1,0:T(8,128)} %bitcast.150), calls=%async_computation.3 | async-start | bytes 4194304 | tf_op jit(solution)/shard_map/all_to_all | solution.py:108
  336.2 28.9 %all-to-all-start.2 = ((f32[64,64,128]{2,1,0:T(8,128)}), f32[64,64,128]{2,1,0:T(8,128)}, u32[]{:S(2)}, u32[]{:S(2)}) async-start(f32[64,64,128]{2,1,0:T(8,128)} %bitcast.152), calls=%async_computation.2 | async-start | bytes 4194304 | tf_op jit(solution)/shard_map/all_to_all | solution.py:107
  365.1 6.9 %slice-start.6 = ((s8[8388608]{0:T(1024)(128)(4,1)}), s8[4194304]{0:T(1024)(128)(4,1)S(1)}, s32[]{:S(2)}) async-start(s8[8388608]{0:T(1024)(128)(4,1)} %bitcast.124), calls=%async_computation.16 | async-start | bytes 8388608
  367.0 5.1 slice-start.7
  372.1 8.9 %slice-start.2 = ((s8[8388608]{0:T(1024)(128)(4,1)}), s8[4194304]{0:T(1024)(128)(4,1)S(1)}, s32[]{:S(2)}) async-start(s8[8388608]{0:T(1024)(128)(4,1)} %bitcast.120), calls=%async_computation.12 | async-start | bytes 8388608
  373.7 7.4 %slice-start.3 = ((s8[8388608]{0:T(1024)(128)(4,1)}), s8[4194304]{0:T(1024)(128)(4,1)S(1)}, s32[]{:S(2)}) async-start(s8[8388608]{0:T(1024)(128)(4,1)} %bitcast.120), calls=%async_computation.13 | async-start | bytes 8388608
  387.4 6.5 %copy-start.12 = (f32[16,64,512]{2,1,0:T(8,128)S(1)}, f32[16,64,512]{2,1,0:T(8,128)}, u32[]{:S(2)}) copy-start(f32[16,64,512]{2,1,0:T(8,128)} %copy-done.11) | copy-start | bytes 6291460
  387.4 6.5 %copy-start.14 = (f32[16,64,512]{2,1,0:T(8,128)S(1)}, f32[16,64,512]{2,1,0:T(8,128)}, u32[]{:S(2)}) copy-start(f32[16,64,512]{2,1,0:T(8,128)} %copy-done.13) | copy-start | bytes 6291460
  387.4 6.5 %copy-start.19 = (f32[16,128,512]{2,1,0:T(8,128)S(1)}, f32[16,128,512]{2,1,0:T(8,128)}, u32[]{:S(2)}) copy-start(f32[16,128,512]{2,1,0:T(8,128)} %fusion.40) | copy-start | bytes 12582916
  409.3 28.0 %all-to-all-start.4 = ((f32[4,1,131072]{2,1,0:T(1,128)}), f32[4,1,131072]{2,1,0:T(1,128)S(1)}, u32[]{:S(2)}, u32[]{:S(2)}) async-start(f32[4,1,131072]{2,1,0:T(1,128)} %reshape.48), calls=%async_computation.4 | async-start | bytes 4194304 | tf_op jit(solution)/shard_map/all_to_all | solution.py:88
  438.6 29.1 %all-to-all-start.5 = ((f32[4,1,131072]{2,1,0:T(1,128)}), f32[4,1,131072]{2,1,0:T(1,128)}, u32[]{:S(2)}, u32[]{:S(2)}) async-start(f32[4,1,131072]{2,1,0:T(1,128)} %reshape.50), calls=%async_computation.5 | async-start | bytes 4194304 | tf_op jit(solution)/shard_map/all_to_all | solution.py:89
  487.5 5.4 copy-start.3
  496.7 29.3 %all-to-all-start.6 = ((f32[64,64,128]{2,1,0:T(8,128)}), f32[64,64,128]{2,1,0:T(8,128)}, u32[]{:S(2)}, u32[]{:S(2)}) async-start(f32[64,64,128]{2,1,0:T(8,128)} %bitcast.151), calls=%async_computation.6 | async-start | bytes 4194304 | tf_op jit(solution)/shard_map/all_to_all | solution.py:107
  526.0 68.3 %all-to-all-start.7 = ((f32[64,64,128]{2,1,0:T(8,128)}), f32[64,64,128]{2,1,0:T(8,128)S(1)}, u32[]{:S(2)}, u32[]{:S(2)}) async-start(f32[64,64,128]{2,1,0:T(8,128)} %bitcast.43), calls=%async_computation.7 | async-start | bytes 4194304 | tf_op jit(solution)/shard_map/all_to_all | solution.py:108
  (17 other events, 44.6 us)
Sparse Core Ops, SparseCore 0:
  9.6 84.7 all-gather.4
  96.0 80.5 all-gather.2
where the time goes:
time: 617 us; the launch traced here: 607 us
  waiting for transfers between devices  247 us (40%)
  local copies, waits for them, and re-layouts  101 us (16%)
  matrix products  97.7 us (16%)
  other arithmetic  56.9 us (9%)
  blocking collectives  54.3 us (9%)
  starting transfers between devices  33.6 us (5%)
  between operations  17.2 us (3%)
    all_gather x1, waiting for transfers between devices, on_device(): lax.all_gather(data_imaginary, 'sa', axis=1, tiled=True)  81.9 us
    all_gather x1, waiting for transfers between devices, on_device(): lax.all_gather(data_real, 'sa', axis=1, tiled=True)  74.9 us
    psum x1, blocking collectives, on_device(): totals = lax.psum(jnp.stack(local_sums), ('af', 'sa'))  54.3 us
    dot_general x16, matrix products, highest(): jnp.dot(left, right, precision=lax.Precision.HIGHEST, preferred_element_t...  52.7 us
    unnamed x90, local copies, waits for them, and re-layouts  51.6 us
    all_to_all x2, waiting for transfers between devices, on_device(): lax.all_to_all(freq_real, 'af', split_axis=0, concat_axis=2, tiled=True)  41.8 us
    all_to_all x2, waiting for transfers between devices, on_device(): lax.all_to_all(stepped_real, 'af', split_axis=2, concat_axis=0, tiled=True)  29.1 us
    all_to_all x2, waiting for transfers between devices, on_device(): lax.all_to_all(freq_imaginary, 'af', split_axis=0, concat_axis=2, tiled=T...  16.8 us
  transfers between devices with their start and end apart: 10, of which 9 were waited for; matrix products, arithmetic and copies ran while one was open for 16% of the time, Pallas kernels for 0%

commit v1 on v0

--- a/solution.py
+++ b/solution.py
@@ -1,3 +1,4 @@
+import functools
 import math
 import jax
 import jax.numpy as jnp
@@ -9,6 +10,16 @@
 ITERS = 2
 STEP_LENGTH = 0.02
 THRESHOLD = 0.25
+
+
+def _form_shelves(content, net_axis):
+    y2 = lax.all_to_all(
+        jnp.stack(jnp.split(content, lax.axis_size(net_axis), axis=2), axis=0), net_axis, 0, 0
+    )
+    return jnp.concatenate(y2, axis=0)
+
+
+scan_the_slabs = functools.partial(_form_shelves, net_axis="af")
 
 
 def fourier_tables(row_index, col_index):
@@ -85,7 +96,7 @@
         stepped_real = current_real + STEP_LENGTH * gradient_real
         stepped_imaginary = current_imaginary + STEP_LENGTH * gradient_imaginary
         trace_real, trace_imaginary = (
-            lax.all_to_all(stepped_real, "af", split_axis=2, concat_axis=0, tiled=True),
+            scan_the_slabs(stepped_real),
             lax.all_to_all(stepped_imaginary, "af", split_axis=2, concat_axis=0, tiled=True),
         )
         block_shape = trace_real.shape

time: 617 us -> 595 us (0.964)
  local copies, waits for them, and re-layouts: 101 us -> 63.4 us
  waiting for transfers between devices: 247 us -> 277 us
  other arithmetic: 56.9 us -> 44.2 us
    all_to_all x2, waiting for transfers between devices: 1.08 us -> 30.9 us  [on_device(): lax.all_to_all(stepped_imaginary, 'af', split_axis=2, concat_axis=0, tile...]
    unnamed x90 -> x82, local copies, waits for them, and re-layouts: 51.6 us -> 30.1 us
    all_to_all x2 -> x0, other arithmetic: 15.2 us -> none  [on_device(): lax.all_to_all(stepped_real, 'af', split_axis=2, concat_axis=0, tiled=True)]
    add x2 -> x0, local copies, waits for them, and re-layouts: 9.72 us -> none  [on_device(): stepped_real = current_real + STEP_LENGTH * gradient_real]
    all_to_all x3 -> x0, local copies, waits for them, and re-layouts: 7.19 us -> none  [on_device(): lax.all_to_all(stepped_real, 'af', split_axis=2, concat_axis=0, tiled=True)]
  transfers between devices with their start and end apart: 10 -> 10, of which waited for: 9 -> 9; matrix products, arithmetic and copies ran while one was open for 16% -> 12% of each run, Pallas kernels for 0% -> 0%
where the time goes in v1:
time: 595 us; the launch traced here: 587 us
  waiting for transfers between devices  277 us (47%)
  matrix products  97.7 us (16%)
  local copies, waits for them, and re-layouts  63.4 us (11%)
  blocking collectives  54.1 us (9%)
  other arithmetic  44.2 us (7%)
  starting transfers between devices  33.4 us (6%)
  between operations  17.4 us (3%)
    all_gather x1, waiting for transfers between devices, on_device(): lax.all_gather(data_imaginary, 'sa', axis=1, tiled=True)  81.9 us
    all_gather x1, waiting for transfers between devices, on_device(): lax.all_gather(data_real, 'sa', axis=1, tiled=True)  74.9 us
    psum x1, blocking collectives, on_device(): totals = lax.psum(jnp.stack(local_sums), ('af', 'sa'))  54.1 us
    dot_general x16, matrix products, highest(): jnp.dot(left, right, precision=lax.Precision.HIGHEST, preferred_element_t...  52.7 us
    all_to_all x2, waiting for transfers between devices, on_device(): lax.all_to_all(freq_real, 'af', split_axis=0, concat_axis=2, tiled=True)  41.7 us
    all_to_all x2, waiting for transfers between devices, on_device(): lax.all_to_all(stepped_imaginary, 'af', split_axis=2, concat_axis=0, tile...  30.9 us
    unnamed x82, local copies, waits for them, and re-layouts  30.1 us
    all_to_all x2, waiting for transfers between devices, _form_shelves(): lax.all_to_all(jnp.stack(jnp.split(content, lax.axis_size(net_axis), axis...  29.1 us
  transfers between devices with their start and end apart: 10, of which 9 were waited for; matrix products, arithmetic and copies ran while one was open for 12% of the time, Pallas kernels for 0%

profile of v1, /device:TPU:0, one launch (start us, length us, event | category | flops | bytes accessed | tf_op | source)
XLA Modules:
  0.0 586.8 jit_solution(15857278290643605927)
XLA Ops:
  12.5 81.9 %all-gather.5.cloned.1.call-done = bf16[16,512,512]{2,1,0:T(8,128)(2,1)} async-done(((bf16[16,64,512]{2,1,0:T(8,128)(2,1)}), bf16[16,512,512]{2,1,0:T(8,128)(2,1)}) %all-gather.5.cloned.1.call-update) | async-done | bytes 8388624 | tf_op jit(solution)/shard_map/all_gather | solution.py:58
  94.4 7.3 %fusion.46 = f32[16,128,512]{2,1,0:T(8,128)} fusion(bf16[16,512,512]{2,1,0:T(8,128)(2,1)} %all-gather.5.cloned.1.call-done, bf16[16,64,512]{2,1,0:T(8,128)(2,1)} %convert_element_type.67, bf16[16,64,512]{2,1,0:T(8,128)(2,1)} %convert_element_type.66), kind=kOutput, calls=%fused_computation.90 | convolution fusion | flops 1077936128 | bytes 14680064 | tf_op jit(solution)/shard_map/frk,fkc->frc/dot_general | solution.py:66
  101.6 74.9 %all-gather.3.cloned.1.call-done = bf16[16,512,512]{2,1,0:T(8,128)(2,1)} async-done(((bf16[16,64,512]{2,1,0:T(8,128)(2,1)}), bf16[16,512,512]{2,1,0:T(8,128)(2,1)}) %all-gather.3.cloned.1.call-update) | async-done | bytes 8388624 | tf_op jit(solution)/shard_map/all_gather | solution.py:57
  176.5 5.4 fusion.47
  189.1 6.8 %fusion.44 = f32[16,128,512]{2,1,0:T(8,128)} fusion(bf16[16,512,512]{2,1,0:T(8,128)(2,1)S(1)} %bitcast.127, bf16[16,64,512]{2,1,0:T(8,128)(2,1)} %convert_element_type.70, bf16[16,64,512]{2,1,0:T(8,128)(2,1)} %convert_element_type.69), kind=kOutput, calls=%fused_computation.88 | convolution fusion | flops 1077936128 | bytes 14680064 | tf_op jit(solution)/shard_map/frk,fjk->frj/dot_general | solution.py:87
  195.9 6.5 %fusion.45 = f32[16,128,512]{2,1,0:T(8,128)} fusion(bf16[16,512,512]{2,1,0:T(8,128)(2,1)S(1)} %bitcast.131, bf16[16,64,512]{2,1,0:T(8,128)(2,1)} %convert_element_type.70, bf16[16,64,512]{2,1,0:T(8,128)(2,1)} %convert_element_type.69), kind=kOutput, calls=%fused_computation.89 | convolution fusion | flops 1077936128 | bytes 14680064 | tf_op jit(solution)/shard_map/frk,fjk->frj/dot_general | solution.py:84
  202.5 5.5 fusion.24
  213.4 4.9 copy.17
  218.2 5.5 reshape.34
  223.7 15.1 %all-to-all-done = f32[4,16,64,128]{3,2,1,0:T(8,128)S(1)} async-done(((f32[4,16,64,128]{3,2,1,0:T(8,128)}), f32[4,16,64,128]{3,2,1,0:T(8,128)S(1)}, u32[]{:S(2)}, u32[]{:S(2)}) %all-to-all-start) | async-done | bytes 2097184 | tf_op jit(solution)/shard_map/all_to_all | solution.py:16
  238.9 4.6 all-to-all-start.1
  252.3 15.7 %all-to-all-done.1 = f32[4,1,131072]{2,1,0:T(1,128)} async-done(((f32[4,1,131072]{2,1,0:T(1,128)}), f32[4,1,131072]{2,1,0:T(1,128)}, u32[]{:S(2)}, u32[]{:S(2)}) %all-to-all-start.1) | async-done | bytes 2097184 | tf_op jit(solution)/shard_map/all_to_all | solution.py:100
  268.6 7.8 %reduce = f32[4,131072]{1,0:T(4,128)S(1)} reduce(f32[4,1,131072]{2,1,0:T(1,128)} %all-to-all-done.1, f32[]{:T(128)} %broadcast.92), dimensions={1}, to_apply=%all_to_all.81.reduce_sub_computation | reduce | bytes 4194308 | tf_op jit(solution)/shard_map/all_to_all | solution.py:100
  283.8 4.9 clamp_subtract_fusion.2
  309.4 16.7 %all-to-all-done.3 = f32[64,64,128]{2,1,0:T(8,128)S(1)} async-done(((f32[64,64,128]{2,1,0:T(8,128)}), f32[64,64,128]{2,1,0:T(8,128)S(1)}, u32[]{:S(2)}, u32[]{:S(2)}) %all-to-all-start.3) | async-done | bytes 2097184 | tf_op jit(solution)/shard_map/all_to_all | solution.py:119
  326.1 4.4 all-to-all-start.2
  331.8 23.3 %all-to-all-done.2 = f32[64,64,128]{2,1,0:T(8,128)} async-done(((f32[64,64,128]{2,1,0:T(8,128)}), f32[64,64,128]{2,1,0:T(8,128)}, u32[]{:S(2)}, u32[]{:S(2)}) %all-to-all-start.2) | async-done | bytes 2097184 | tf_op jit(solution)/shard_map/all_to_all | solution.py:118
  357.0 4.9 fusion.42
  371.0 6.4 %fusion.40 = f32[16,128,512]{2,1,0:T(8,128)} fusion(bf16[16,512,512]{2,1,0:T(8,128)(2,1)S(1)} %bitcast.129, bf16[16,64,512]{2,1,0:T(8,128)(2,1)} %convert_element_type.74, bf16[16,64,512]{2,1,0:T(8,128)(2,1)} %convert_element_type.73), kind=kOutput, calls=%fused_computation.84 | convolution fusion | flops 1077936128 | bytes 14680064 | tf_op jit(solution)/shard_map/frk,fjk->frj/dot_general | solution.py:87
  377.4 6.5 %fusion.41 = f32[16,128,512]{2,1,0:T(8,128)} fusion(bf16[16,512,512]{2,1,0:T(8,128)(2,1)S(1)} %bitcast.133, bf16[16,64,512]{2,1,0:T(8,128)(2,1)} %convert_element_type.74, bf16[16,64,512]{2,1,0:T(8,128)(2,1)} %convert_element_type.73), kind=kOutput, calls=%fused_computation.85 | convolution fusion | flops 1077936128 | bytes 14680064 | tf_op jit(solution)/shard_map/frk,fjk->frj/dot_general | solution.py:84
  383.9 4.7 bitcast_add_fusion
  394.0 4.9 copy.21
  398.8 5.5 reshape.36
  404.3 14.0 %all-to-all-done.4 = f32[4,16,64,128]{3,2,1,0:T(8,128)S(1)} async-done(((f32[4,16,64,128]{3,2,1,0:T(8,128)}), f32[4,16,64,128]{3,2,1,0:T(8,128)S(1)}, u32[]{:S(2)}, u32[]{:S(2)}) %all-to-all-start.4) | async-done | bytes 2097184 | tf_op jit(solution)/shard_map/all_to_all | solution.py:16
  418.3 4.9 all-to-all-start.5
  427.6 4.4 fusion.8
  432.0 15.2 %all-to-all-done.5 = f32[4,1,131072]{2,1,0:T(1,128)} async-done(((f32[4,1,131072]{2,1,0:T(1,128)}), f32[4,1,131072]{2,1,0:T(1,128)}, u32[]{:S(2)}, u32[]{:S(2)}) %all-to-all-start.5) | async-done | bytes 2097184 | tf_op jit(solution)/shard_map/all_to_all | solution.py:100
  447.2 7.8 %reduce.1 = f32[4,131072]{1,0:T(4,128)S(1)} reduce(f32[4,1,131072]{2,1,0:T(1,128)} %all-to-all-done.5, f32[]{:T(128)} %broadcast.92), dimensions={1}, to_apply=%all_to_all.93.reduce_sub_computation | reduce | bytes 4194308 | tf_op jit(solution)/shard_map/all_to_all | solution.py:100
  462.2 5.0 clamp_subtract_fusion
  476.4 4.8 all-to-all-start.6
  487.2 18.4 %all-to-all-done.6 = f32[64,64,128]{2,1,0:T(8,128)} async-done(((f32[64,64,128]{2,1,0:T(8,128)}), f32[64,64,128]{2,1,0:T(8,128)}, u32[]{:S(2)}, u32[]{:S(2)}) %all-to-all-start.6) | async-done | bytes 2097184 | tf_op jit(solution)/shard_map/all_to_all | solution.py:118
  511.9 54.1 %psum.7 = f32[2]{0:T(128)S(1)} all-reduce(f32[2]{0:T(128)S(1)} %pad_maximum_fusion.14), channel_id=1, replica_groups=mesh['af'=4,'sa'=8] {'af','sa'}, use_global_device_ids=true, to_apply=%region_4.5 | all-reduce | flops 2 | bytes 16 | tf_op jit(solution)/shard_map/psum | solution.py:121
  (130 shorter events, 116.9 us)
Async XLA Ops:
  7.2 87.2 %all-gather.5.cloned.1.call-start = ((), (), s32[]{:S(2)}) async-start(), calls=%async_computation.9 | async-start | bytes 9437184 | tf_op jit(solution)/shard_map/all_gather | solution.py:58
  7.9 168.6 %all-gather.3.cloned.1.call-start = ((), (), s32[]{:S(2)}) async-start(), calls=%async_computation.8 | async-start | bytes 9437184 | tf_op jit(solution)/shard_map/all_gather | solution.py:57
  101.6 80.3 %copy-start.27 = (f32[16]{0:T(128)S(1)}, f32[16]{0:T(128)}, u32[]{:S(2)}) copy-start(f32[16]{0:T(128)} %param.9) | copy-start | bytes 196
  101.6 80.3 %copy-start.28 = (f32[16]{0:T(128)S(1)}, f32[16]{0:T(128)}, u32[]{:S(2)}) copy-start(f32[16]{0:T(128)} %param.8) | copy-start | bytes 196
  176.5 5.5 copy-start
  176.5 5.9 %copy-start.9 = (f32[16,64,512]{2,1,0:T(8,128)S(1)}, f32[16,64,512]{2,1,0:T(8,128)}, u32[]{:S(2)}) copy-start(f32[16,64,512]{2,1,0:T(8,128)} %param.10) | copy-start | bytes 6291460
  176.5 6.1 %copy-start.21 = (bf16[16,64,512]{2,1,0:T(8,128)(2,1)S(1)}, bf16[16,64,512]{2,1,0:T(8,128)(2,1)}, u32[]{:S(2)}) copy-start(bf16[16,64,512]{2,1,0:T(8,128)(2,1)} %param.7) | copy-start | bytes 3145732
  176.5 6.4 %copy-start.23 = (bf16[16,64,512]{2,1,0:T(8,128)(2,1)S(1)}, bf16[16,64,512]{2,1,0:T(8,128)(2,1)}, u32[]{:S(2)}) copy-start(bf16[16,64,512]{2,1,0:T(8,128)(2,1)} %param.6) | copy-start | bytes 3145732
  176.5 12.5 %slice-start = ((s8[8388608]{0:T(1024)(128)(4,1)}), s8[4194304]{0:T(1024)(128)(4,1)S(1)}, s32[]{:S(2)}) async-start(s8[8388608]{0:T(1024)(128)(4,1)} %bitcast.126), calls=%async_computation.10 | async-start | bytes 8388608
  182.9 6.1 %slice-start.1 = ((s8[8388608]{0:T(1024)(128)(4,1)}), s8[4194304]{0:T(1024)(128)(4,1)S(1)}, s32[]{:S(2)}) async-start(s8[8388608]{0:T(1024)(128)(4,1)} %bitcast.126), calls=%async_computation.11 | async-start | bytes 8388608
  187.9 8.0 %slice-start.4 = ((s8[8388608]{0:T(1024)(128)(4,1)}), s8[4194304]{0:T(1024)(128)(4,1)S(1)}, s32[]{:S(2)}) async-start(s8[8388608]{0:T(1024)(128)(4,1)} %bitcast.130), calls=%async_computation.14 | async-start | bytes 8388608
  189.1 6.9 %slice-start.5 = ((s8[8388608]{0:T(1024)(128)(4,1)}), s8[4194304]{0:T(1024)(128)(4,1)S(1)}, s32[]{:S(2)}) async-start(s8[8388608]{0:T(1024)(128)(4,1)} %bitcast.130), calls=%async_computation.15 | async-start | bytes 8388608
  195.9 6.6 %copy-start.10 = (f32[16,64,512]{2,1,0:T(8,128)S(1)}, f32[16,64,512]{2,1,0:T(8,128)}, u32[]{:S(2)}) copy-start(f32[16,64,512]{2,1,0:T(8,128)} %param.10) | copy-start | bytes 6291460
  195.9 6.6 %copy-start.16 = (f32[16,64,512]{2,1,0:T(8,128)S(1)}, f32[16,64,512]{2,1,0:T(8,128)}, u32[]{:S(2)}) copy-start(f32[16,64,512]{2,1,0:T(8,128)} %copy-done.15) | copy-start | bytes 6291460
  195.9 6.6 %copy-start.18 = (f32[16,64,512]{2,1,0:T(8,128)S(1)}, f32[16,64,512]{2,1,0:T(8,128)}, u32[]{:S(2)}) copy-start(f32[16,64,512]{2,1,0:T(8,128)} %copy-done.17) | copy-start | bytes 6291460
  209.7 29.1 %all-to-all-start = ((f32[4,16,64,128]{3,2,1,0:T(8,128)}), f32[4,16,64,128]{3,2,1,0:T(8,128)S(1)}, u32[]{:S(2)}, u32[]{:S(2)}) async-start(f32[4,16,64,128]{3,2,1,0:T(8,128)} %pad_maximum_fusion.2), calls=%async_computation | async-start | bytes 4194304 | tf_op jit(solution)/shard_map/all_to_all | solution.py:16
  238.9 29.1 %all-to-all-start.1 = ((f32[4,1,131072]{2,1,0:T(1,128)}), f32[4,1,131072]{2,1,0:T(1,128)}, u32[]{:S(2)}, u32[]{:S(2)}) async-start(f32[4,1,131072]{2,1,0:T(1,128)} %reshape.34), calls=%async_computation.1 | async-start | bytes 4194304 | tf_op jit(solution)/shard_map/all_to_all | solution.py:100
  292.0 6.0 %copy-start.7 = (f32[64,8192]{1,0:T(8,128)}, f32[64,8192]{1,0:T(8,128)S(1)}, u32[]{:S(2)}) copy-start(f32[64,8192]{1,0:T(8,128)S(1)} %clamp_subtract_fusion.3) | copy-start | bytes 6291460
  298.0 28.1 %all-to-all-start.3 = ((f32[64,64,128]{2,1,0:T(8,128)}), f32[64,64,128]{2,1,0:T(8,128)S(1)}, u32[]{:S(2)}, u32[]{:S(2)}) async-start(f32[64,64,128]{2,1,0:T(8,128)} %bitcast.154), calls=%async_computation.3 | async-start | bytes 4194304 | tf_op jit(solution)/shard_map/all_to_all | solution.py:119
  326.1 28.9 %all-to-all-start.2 = ((f32[64,64,128]{2,1,0:T(8,128)}), f32[64,64,128]{2,1,0:T(8,128)}, u32[]{:S(2)}, u32[]{:S(2)}) async-start(f32[64,64,128]{2,1,0:T(8,128)} %bitcast.156), calls=%async_computation.2 | async-start | bytes 4194304 | tf_op jit(solution)/shard_map/all_to_all | solution.py:118
  355.1 6.8 %slice-start.6 = ((s8[8388608]{0:T(1024)(128)(4,1)}), s8[4194304]{0:T(1024)(128)(4,1)S(1)}, s32[]{:S(2)}) async-start(s8[8388608]{0:T(1024)(128)(4,1)} %bitcast.132), calls=%async_computation.16 | async-start | bytes 8388608
  357.0 5.1 slice-start.7
  362.1 9.0 %slice-start.2 = ((s8[8388608]{0:T(1024)(128)(4,1)}), s8[4194304]{0:T(1024)(128)(4,1)S(1)}, s32[]{:S(2)}) async-start(s8[8388608]{0:T(1024)(128)(4,1)} %bitcast.128), calls=%async_computation.12 | async-start | bytes 8388608
  363.6 7.4 %slice-start.3 = ((s8[8388608]{0:T(1024)(128)(4,1)}), s8[4194304]{0:T(1024)(128)(4,1)S(1)}, s32[]{:S(2)}) async-start(s8[8388608]{0:T(1024)(128)(4,1)} %bitcast.128), calls=%async_computation.13 | async-start | bytes 8388608
  377.4 6.5 %copy-start.12 = (f32[16,64,512]{2,1,0:T(8,128)S(1)}, f32[16,64,512]{2,1,0:T(8,128)}, u32[]{:S(2)}) copy-start(f32[16,64,512]{2,1,0:T(8,128)} %copy-done.11) | copy-start | bytes 6291460
  377.4 6.5 %copy-start.14 = (f32[16,64,512]{2,1,0:T(8,128)S(1)}, f32[16,64,512]{2,1,0:T(8,128)}, u32[]{:S(2)}) copy-start(f32[16,64,512]{2,1,0:T(8,128)} %copy-done.13) | copy-start | bytes 6291460
  377.4 6.5 %copy-start.19 = (f32[16,128,512]{2,1,0:T(8,128)S(1)}, f32[16,128,512]{2,1,0:T(8,128)}, u32[]{:S(2)}) copy-start(f32[16,128,512]{2,1,0:T(8,128)} %fusion.40) | copy-start | bytes 12582916
  390.3 28.0 %all-to-all-start.4 = ((f32[4,16,64,128]{3,2,1,0:T(8,128)}), f32[4,16,64,128]{3,2,1,0:T(8,128)S(1)}, u32[]{:S(2)}, u32[]{:S(2)}) async-start(f32[4,16,64,128]{3,2,1,0:T(8,128)} %pad_maximum_fusion.5), calls=%async_computation.4 | async-start | bytes 4194304 | tf_op jit(solution)/shard_map/all_to_all | solution.py:16
  418.3 28.9 %all-to-all-start.5 = ((f32[4,1,131072]{2,1,0:T(1,128)}), f32[4,1,131072]{2,1,0:T(1,128)}, u32[]{:S(2)}, u32[]{:S(2)}) async-start(f32[4,1,131072]{2,1,0:T(1,128)} %reshape.36), calls=%async_computation.5 | async-start | bytes 4194304 | tf_op jit(solution)/shard_map/all_to_all | solution.py:100
  467.2 5.4 copy-start.3
  476.4 29.2 %all-to-all-start.6 = ((f32[64,64,128]{2,1,0:T(8,128)}), f32[64,64,128]{2,1,0:T(8,128)}, u32[]{:S(2)}, u32[]{:S(2)}) async-start(f32[64,64,128]{2,1,0:T(8,128)} %bitcast.155), calls=%async_computation.6 | async-start | bytes 4194304 | tf_op jit(solution)/shard_map/all_to_all | solution.py:118
  505.7 68.3 %all-to-all-start.7 = ((f32[64,64,128]{2,1,0:T(8,128)}), f32[64,64,128]{2,1,0:T(8,128)S(1)}, u32[]{:S(2)}, u32[]{:S(2)}) async-start(f32[64,64,128]{2,1,0:T(8,128)} %bitcast.47), calls=%async_computation.7 | async-start | bytes 4194304 | tf_op jit(solution)/shard_map/all_to_all | solution.py:119
  (15 other events, 42.0 us)
Sparse Core Ops, SparseCore 0:
  9.6 84.7 all-gather.4
  96.0 80.5 all-gather.2
